TPU v7x, 128 devices: a whole 4x4x4 slice. The times are simulated.
128 devices in a mesh: section: 16 (over z, x_hi, core), tm: 8 (over y, x_lo).
Axes of the slice: x: 4 (x_hi: 2, x_lo: 2; x = x_hi * 2 + x_lo), y: 4, z: 4, core: 2. Of those that a mesh axis runs over, the one named last changes fastest.
Arguments:
- frames: bfloat16 [4, 512, 1024], P(None, 'tm'), may hold values from -6 to 6, as said below
- lengths: int32 [4], replicated, may hold values from 128 to 512
- ffn_gain: float32 [16, 1024], P('section'), may hold values from 0.1 to 1.9
- ffn_up: bfloat16 [16, 1024, 2048], P('section'), may hold values from -0.1875 to 0.1875
- ffn_down: bfloat16 [16, 2048, 1024], P('section'), may hold values from -0.125 to 0.125
- attn_gain: float32 [16, 1024], P('section'), may hold values from 0.1 to 1.9
- query_weight: bfloat16 [16, 1024, 1024], P('section'), may hold values from -8 to 8
- key_weight: bfloat16 [16, 1024, 1024], P('section'), may hold values from -0.1875 to 0.1875
- value_weight: bfloat16 [16, 1024, 1024], P('section'), may hold values from -0.1875 to 0.1875
- out_weight: bfloat16 [16, 1024, 1024], P('section'), may hold values from -0.1875 to 0.1875
- conv_gain: float32 [16, 1024], P('section'), may hold values from 0.1 to 1.9
- expand_weight: bfloat16 [16, 1024, 2048], P('section'), may hold values from -0.1875 to 0.1875
- depth_weight: float32 [16, 31, 1024], P('section'), may hold values from -1 to 1
- depth_gain: float32 [16, 1024], P('section'), may hold values from 0.1 to 1.9
- norm_shift: float32 [16, 1024], P('section'), may hold values from -0.5 to 0.5
- shrink_weight: bfloat16 [16, 1024, 1024], P('section'), may hold values from -0.1875 to 0.1875
- final_gain: float32 [16, 1024], P('section'), may hold values from 0.1 to 1.9
Outputs:
- hidden_states: bfloat16 [16, 4, 512, 1024], P('section', None, 'tm')
Inputs may be any that keep to these rules, and one draw needn't show every extreme that they name: `frames`: input features of order one.
All inputs are finite; a program needn't handle non-finite values.
Results may differ from a plain program's by a relative error of at most 0.02.
Values may be sent and summed in bfloat16 or wider, within the bound.
A program may use at most 128 MiB of HBM per device.

v0:
```python
import math
import jax
import jax.numpy as jnp
from jax import lax
from jax.sharding import PartitionSpec as P

HEADS = 16
EPS = 1e-05


def extended(shard, sides, width):
    for axis, dim in sides:
        peers, length = (lax.axis_size(axis), shard.shape[dim])
        up = [(i, (i + 1) % peers) for i in range(peers - 1)]
        down = [(j, i) for i, j in up]
        last = lax.slice_in_dim(shard, length - width, length, axis=dim)
        initial = lax.slice_in_dim(shard, 0, width, axis=dim)
        before = lax.ppermute(last, axis, up)
        after = lax.ppermute(initial, axis, down)
        shard = jnp.concatenate([before, shard, after], axis=dim)
    return shard


def passed_along(shard, axis, by):
    peers = lax.axis_size(axis)
    pairs = [(i, i + by) for i in range(peers) if 0 <= i + by < peers]
    return lax.ppermute(shard, axis, pairs)


def normalize(value, gain):
    mean = jnp.mean(value, axis=-1, keepdims=True)
    centred = value - mean
    spread = jnp.mean(centred * centred, axis=-1, keepdims=True)
    return centred * lax.rsqrt(spread + EPS) * gain


def body(
    frames,
    lengths,
    ffn_gain,
    ffn_up,
    ffn_down,
    attn_gain,
    query_weight,
    key_weight,
    value_weight,
    out_weight,
    conv_gain,
    expand_weight,
    depth_weight,
    depth_gain,
    norm_shift,
    shrink_weight,
    final_gain,
):
    sections = lax.axis_size("section")
    groups = lax.axis_size("tm")
    section_index = lax.axis_index("section")
    group_index = lax.axis_index("tm")
    micro, rows, width = frames.shape
    whole = rows * groups
    heads = HEADS
    head = width // heads
    kernel = depth_weight.shape[1]
    rim = kernel // 2
    scale = 1.0 / math.sqrt(head)
    gain_ffn = ffn_gain[0]
    w_up = ffn_up[0]
    w_down = ffn_down[0]
    gain_a = attn_gain[0]
    w_query = query_weight[0]
    w_key = key_weight[0]
    w_value = value_weight[0]
    w_out = out_weight[0]
    gain_c = conv_gain[0]
    w_expand = expand_weight[0]
    w_depth = depth_weight[0]
    gain_depth = depth_gain[0]
    bias_depth = norm_shift[0]
    w_shrink = shrink_weight[0]
    gain_f = final_gain[0]
    local_pos = group_index * rows + jnp.arange(rows, dtype=jnp.int32)
    zero_rows = jnp.zeros((rows, width), jnp.bfloat16)
    zero_mid = jnp.zeros((rows, width), jnp.float32)

    def tick(step, carry):
        incoming, gathered = carry
        offset = step - section_index
        active = (offset >= 0) & (offset < micro)
        slot = jnp.clip(offset, 0, micro - 1)
        fresh = lax.dynamic_index_in_dim(frames, slot, 0, keepdims=False)
        inputs = jnp.where(section_index == 0, fresh, incoming)
        length = jnp.sum(jnp.where(jnp.arange(micro, dtype=jnp.int32) == slot, lengths, 0))

        def project():
            ffn_normed = normalize(inputs.astype(jnp.float32), gain_ffn).astype(jnp.bfloat16)
            inner = jax.nn.silu(
                jnp.dot(ffn_normed, w_up, preferred_element_type=jnp.float32)
            ).astype(jnp.bfloat16)
            start = inputs.astype(jnp.float32) + 0.5 * jnp.dot(
                inner, w_down, preferred_element_type=jnp.float32
            )
            normed = normalize(start, gain_a).astype(jnp.bfloat16)
            q_all, k_all, v_all = tuple(
                (
                    jnp.dot(normed, weight, preferred_element_type=jnp.float32).astype(jnp.bfloat16)
                    for weight in (w_query, w_key, w_value)
                )
            )
            return (start, q_all, k_all, v_all)

        start, queries, keys, values = lax.cond(
            active, project, lambda: (zero_mid, zero_rows, zero_rows, zero_rows)
        )
        g_query, g_key, g_value = (
            lax.all_to_all(queries, "tm", split_axis=1, concat_axis=0, tiled=True),
            lax.all_to_all(keys, "tm", split_axis=1, concat_axis=0, tiled=True),
            lax.all_to_all(values, "tm", split_axis=1, concat_axis=0, tiled=True),
        )
        local_heads = g_query.shape[1] // head
        span = 512

        def attend_groups():
            seen = jnp.arange(whole, dtype=jnp.int32) < length
            k_heads = g_key.reshape(whole, local_heads, head)
            v_heads = g_value.reshape(whole, local_heads, head)
            q_blocks = g_query.reshape(whole // span, span, local_heads, head)

            def one_block(q_block):
                scores = (
                    jnp.einsum("qgd,kgd->gqk", q_block, k_heads, preferred_element_type=jnp.float32)
                    * scale
                )
                scores = jnp.where(seen[None, None, :], scores, -1e30)
                peak = jnp.max(scores, axis=-1, keepdims=True)
                weights_h = jnp.exp(scores - peak)
                total = jnp.sum(weights_h, axis=-1, keepdims=True)
                mixed = jnp.einsum(
                    "gqk,kgd->qgd",
                    weights_h.astype(jnp.bfloat16),
                    v_heads,
                    preferred_element_type=jnp.float32,
                )
                mixed = mixed / jnp.transpose(total, (1, 0, 2))
                return mixed.astype(jnp.bfloat16).reshape(span, local_heads * head)

            return lax.map(one_block, q_blocks).reshape(whole, local_heads * head)

        grouped = lax.cond(
            active, attend_groups, lambda: jnp.zeros((whole, local_heads * head), jnp.bfloat16)
        )
        context = lax.all_to_all(grouped, "tm", split_axis=0, concat_axis=1, tiled=True)

        def conv_front():
            mid = start + jnp.dot(context, w_out, preferred_element_type=jnp.float32)
            conv_in = normalize(mid, gain_c).astype(jnp.bfloat16)
            expanded = jnp.dot(conv_in, w_expand, preferred_element_type=jnp.float32)
            keep = (local_pos < length).astype(jnp.float32)
            glu = expanded[:, :width] * jax.nn.sigmoid(expanded[:, width:]) * keep[:, None]
            return (mid, glu.astype(jnp.bfloat16))

        mid, glu = lax.cond(active, conv_front, lambda: (zero_mid, zero_rows))
        padded = extended(glu, (("tm", 0),), rim)

        def conv_back():
            widened = padded.astype(jnp.float32)
            depth = jnp.zeros((rows, width), jnp.float32)
            for offset_j in range(kernel):
                depth = depth + widened[offset_j : offset_j + rows] * w_depth[offset_j]
            shifted = normalize(depth, gain_depth) + bias_depth
            swished = (shifted * jax.nn.sigmoid(shifted)).astype(jnp.bfloat16)
            closing = mid + jnp.dot(swished, w_shrink, preferred_element_type=jnp.float32)
            return normalize(closing, gain_f).astype(jnp.bfloat16)

        result = lax.cond(active, conv_back, lambda: zero_rows)
        previous = lax.dynamic_index_in_dim(gathered, slot, 0, keepdims=False)
        gathered = lax.dynamic_update_index_in_dim(
            gathered, jnp.where(active, result, previous), slot, 0
        )
        incoming = passed_along(result, "section", 1)
        return (incoming, gathered)

    start_outs = jnp.zeros((micro, rows, width), jnp.bfloat16)
    final_in, hidden_states = lax.fori_loop(0, micro + sections - 1, tick, (zero_rows, start_outs))
    return hidden_states[None]


def solution(mesh):
    return jax.shard_map(
        body,
        mesh=mesh,
        in_specs=(
            P(None, "tm", None),
            P(),
            P("section", None),
            P("section", None, None),
            P("section", None, None),
            P("section", None),
            P("section", None, None),
            P("section", None, None),
            P("section", None, None),
            P("section", None, None),
            P("section", None),
            P("section", None, None),
            P("section", None, None),
            P("section", None),
            P("section", None),
            P("section", None, None),
            P("section", None),
        ),
        out_specs=P("section", None, "tm", None),
        check_vma=False,
    )
```

profile of v0, /device:TPU:109, one launch (start us, length us, event | category | flops | bytes accessed | tf_op | source)
XLA Modules:
  0.0 1492.9 jit_solution(9825759738350076696)
XLA Ops:
  2.5 1490.5 %while.21 = (s32[]{:T(128)}, bf16[64,1024]{1,0:T(8,128)(2,1)S(1)}, bf16[4,64,1024]{2,1,0:T(8,128)(2,1)}, s32[]{:T(128)}, s32[4]{0:T(128)}, /*index=5*/pred[]{:T(...) while((s32[]{:T(128)}, bf16[64,1024]{1,0:T(8,128)(2,1)S(1)}, ...), condition=%wide.region_22.23_spmd.clone, body=%wide.region_0.22_spmd.clone.sunk | while | flops 1626031104 | bytes 78909456 | solution.py:184
  3.3 5.0 all-to-all-start
  12.5 4.7 all-to-all-start.1
  51.9 7.7 collective-permute-done.2
  67.9 4.6 all-to-all-start.1
  107.4 12.2 collective-permute-done.2
  127.8 4.6 all-to-all-start.1
  167.2 12.2 collective-permute-done.2
  187.7 4.6 all-to-all-start.1
  227.1 12.2 collective-permute-done.2
  247.6 4.6 all-to-all-start.1
  287.0 12.2 collective-permute-done.2
  307.4 4.6 all-to-all-start.1
  346.9 12.2 collective-permute-done.2
  406.7 12.2 collective-permute-done.2
  427.2 4.6 all-to-all-start.1
  466.6 12.2 collective-permute-done.2
  487.0 4.6 all-to-all-start.1
  526.5 12.2 collective-permute-done.2
  546.9 4.6 all-to-all-start.1
  586.3 12.2 collective-permute-done.2
  606.8 4.6 all-to-all-start.1
  646.2 12.5 collective-permute-done.2
  667.1 4.6 all-to-all-start.1
  706.6 12.5 collective-permute-done.2
  727.5 4.6 all-to-all-start.1
  766.9 12.4 collective-permute-done.2
  787.6 4.6 all-to-all-start.1
  827.0 12.2 collective-permute-done.2
  847.4 4.6 all-to-all-start.1
  886.9 279.0 %collective-permute-done.2 = bf16[64,1024]{1,0:T(8,128)(2,1)S(1)} collective-permute-done((bf16[64,1024]{1,0:T(8,128)(2,1)S(1)}, bf16[64,1024]{1,0:T(8,128)(2,1)S(1)}, u32[]{:S(2)}, u32[]{:S(2)}) %collective-permute-start.2) | collective-permute-done | bytes 131104 | tf_op jit(solution)/shard_map/while/body/eval_jaxpr/ppermute | solution.py:27
  1165.8 10.7 conditional.12
  1167.1 5.2 fusion.89
  1215.0 8.2 conditional.14
  1237.5 13.3 collective-permute-done.2
  1250.8 10.7 conditional.12
  1252.1 5.2 fusion.89
  1299.9 8.2 conditional.14
  1322.4 13.3 collective-permute-done.2
  1335.7 10.7 conditional.12
  1337.0 5.2 fusion.89
  1354.6 4.6 all-to-all-start.1
  1384.8 8.2 conditional.14
  1407.3 12.8 collective-permute-done.2
  1420.1 10.7 conditional.12
  1421.4 5.2 fusion.89
  1439.0 4.6 all-to-all-start.1
  1469.2 8.2 conditional.14
  (1066 shorter events, 938.9 us)
Async XLA Ops:
  3.3 9.2 all-to-all-start
  12.5 8.9 all-to-all-start.1
  21.4 8.8 all-to-all-start.2
  49.9 9.7 collective-permute-start.2
  67.9 8.9 all-to-all-start.1
  76.8 8.8 all-to-all-start.2
  105.4 14.2 collective-permute-start.2
  127.8 8.9 all-to-all-start.1
  136.7 8.8 all-to-all-start.2
  165.2 14.2 collective-permute-start.2
  187.7 8.9 all-to-all-start.1
  196.5 8.8 all-to-all-start.2
  225.1 14.2 collective-permute-start.2
  247.6 8.9 all-to-all-start.1
  256.4 8.8 all-to-all-start.2
  285.0 14.2 collective-permute-start.2
  307.4 8.9 all-to-all-start.1
  316.3 8.8 all-to-all-start.2
  344.9 14.2 collective-permute-start.2
  367.3 8.9 all-to-all-start.1
  376.2 8.8 all-to-all-start.2
  404.7 14.2 collective-permute-start.2
  427.2 8.9 all-to-all-start.1
  436.0 8.8 all-to-all-start.2
  464.6 14.2 collective-permute-start.2
  487.0 8.9 all-to-all-start.1
  495.9 8.8 all-to-all-start.2
  524.5 14.2 collective-permute-start.2
  546.9 8.9 all-to-all-start.1
  584.4 14.2 collective-permute-start.2
  606.8 8.9 all-to-all-start.1
  644.2 14.5 collective-permute-start.2
  667.1 8.9 all-to-all-start.1
  704.6 14.5 collective-permute-start.2
  727.5 8.9 all-to-all-start.1
  764.9 14.4 collective-permute-start.2
  787.6 8.9 all-to-all-start.1
  825.0 14.2 collective-permute-start.2
  847.4 8.9 all-to-all-start.1
  884.9 280.9 %collective-permute-start.2 = (bf16[64,1024]{1,0:T(8,128)(2,1)S(1)}, bf16[64,1024]{1,0:T(8,128)(2,1)S(1)}, u32[]{:S(2)}, u32[]{:S(2)}) collective-permute-start(bf16[64,1024]{1,0:T(8,128)(2,1)S(1)} %get-tuple-element.1026), channel_id=1, source_target_pairs={{0,8},{8,16},{16,24},{24,32},{32,40},{40,48},{48,56},{56,64},{64,7... | collective-permute-start | bytes 393224 | tf_op jit(solution)/shard_map/while/body/eval_jaxpr/ppermute | solution.py:27
  1184.8 8.9 all-to-all-start.1
  1193.6 8.9 all-to-all-start.2
  1235.5 15.3 %collective-permute-start.2 = (bf16[64,1024]{1,0:T(8,128)(2,1)S(1)}, bf16[64,1024]{1,0:T(8,128)(2,1)S(1)}, u32[]{:S(2)}, u32[]{:S(2)}) collective-permute-start(bf16[64,1024]{1,0:T(8,128)(2,1)S(1)} %get-tuple-element.1026), channel_id=1, source_target_pairs={{0,8},{8,16},{16,24},{24,32},{32,40},{40,48},{48,56},{56,64},{64,7... | collective-permute-start | bytes 393224 | tf_op jit(solution)/shard_map/while/body/eval_jaxpr/ppermute | solution.py:27
  1269.7 8.9 all-to-all-start.1
  1320.4 15.3 %collective-permute-start.2 = (bf16[64,1024]{1,0:T(8,128)(2,1)S(1)}, bf16[64,1024]{1,0:T(8,128)(2,1)S(1)}, u32[]{:S(2)}, u32[]{:S(2)}) collective-permute-start(bf16[64,1024]{1,0:T(8,128)(2,1)S(1)} %get-tuple-element.1026), channel_id=1, source_target_pairs={{0,8},{8,16},{16,24},{24,32},{32,40},{40,48},{48,56},{56,64},{64,7... | collective-permute-start | bytes 393224 | tf_op jit(solution)/shard_map/while/body/eval_jaxpr/ppermute | solution.py:27
  1354.6 8.9 all-to-all-start.1
  1405.3 14.8 collective-permute-start.2
  1439.0 8.9 all-to-all-start.1
  (238 other events, 2423.1 us)
where the time goes:
time: 1500 us; the launch traced here: 1490 us
  waiting for transfers between devices  819 us (55%)
  starting transfers between devices  457 us (30%)
  local copies, waits for them, and re-layouts  89.2 us (6%)
  matrix products  70 us (5%)
  other arithmetic  52.2 us (3%)
    ppermute x19, waiting for transfers between devices, passed_along(): return lax.ppermute(shard, axis, pairs)  487 us
    all_to_all x19, starting transfers between devices, tick(): lax.all_to_all(keys, 'tm', split_axis=1, concat_axis=0, tiled=True)  88.1 us
    all_to_all x19, starting transfers between devices, tick(): lax.all_to_all(values, 'tm', split_axis=1, concat_axis=0, tiled=True)  87.8 us
    all_to_all x19, starting transfers between devices, tick(): lax.all_to_all(grouped, 'tm', split_axis=0, concat_axis=1, tiled=True)  87.8 us
    all_to_all x19, waiting for transfers between devices, tick(): lax.all_to_all(grouped, 'tm', split_axis=0, concat_axis=1, tiled=True)  80.3 us
    all_to_all x19, waiting for transfers between devices, tick(): lax.all_to_all(keys, 'tm', split_axis=1, concat_axis=0, tiled=True)  67.6 us
    ppermute x19, starting transfers between devices, extended(): after = lax.ppermute(initial, axis, down)  67.1 us
    all_to_all x19, waiting for transfers between devices, tick(): lax.all_to_all(values, 'tm', split_axis=1, concat_axis=0, tiled=True)  66.7 us
  transfers between devices with their start and end apart: 133, of which 114 were waited for; matrix products, arithmetic and copies ran while one was open for 5% of the time, Pallas kernels for 0%

commit v1 on v0

--- a/solution.py
+++ b/solution.py
@@ -149,7 +149,9 @@
         grouped = lax.cond(
             active, attend_groups, lambda: jnp.zeros((whole, local_heads * head), jnp.bfloat16)
         )
-        context = lax.all_to_all(grouped, "tm", split_axis=0, concat_axis=1, tiled=True)
+        pieces = jnp.split(grouped, lax.axis_size("tm"), axis=0)
+        incoming_2 = lax.all_to_all(jnp.stack(pieces), "tm", 0, 0)
+        context = jnp.concatenate(incoming_2, axis=1)
 
         def conv_front():
             mid = start + jnp.dot(context, w_out, preferred_element_type=jnp.float32)

time: 1500 us -> 1600 us (1.067)
  local copies, waits for them, and re-layouts: 89.2 us -> 169 us
    while x266 -> x361, local copies, waits for them, and re-layouts: 0.64 us -> 80.3 us
  transfers between devices with their start and end apart: 133 -> 133, of which waited for: 114 -> 114; matrix products, arithmetic and copies ran while one was open for 5% -> 4% of each run, Pallas kernels for 0% -> 0%
where the time goes in v1:
time: 1600 us; the launch traced here: 1580 us
  waiting for transfers between devices  833 us (52%)
  starting transfers between devices  455 us (28%)
  local copies, waits for them, and re-layouts  169 us (11%)
  matrix products  70 us (4%)
  other arithmetic  51.3 us (3%)
    ppermute x19, waiting for transfers between devices, passed_along(): return lax.ppermute(shard, axis, pairs)  499 us
    all_to_all x19, starting transfers between devices, tick(): lax.all_to_all(keys, 'tm', split_axis=1, concat_axis=0, tiled=True)  88.1 us
    all_to_all x19, starting transfers between devices, tick(): lax.all_to_all(values, 'tm', split_axis=1, concat_axis=0, tiled=True)  87.8 us
    all_to_all x19, starting transfers between devices, tick(): incoming_2 = lax.all_to_all(jnp.stack(pieces), 'tm', 0, 0)  87.8 us
    all_to_all x19, waiting for transfers between devices, tick(): incoming_2 = lax.all_to_all(jnp.stack(pieces), 'tm', 0, 0)  80.3 us
    while x361, local copies, waits for them, and re-layouts  80.3 us
    all_to_all x19, waiting for transfers between devices, tick(): lax.all_to_all(keys, 'tm', split_axis=1, concat_axis=0, tiled=True)  67.6 us
    all_to_all x19, waiting for transfers between devices, tick(): lax.all_to_all(values, 'tm', split_axis=1, concat_axis=0, tiled=True)  67.1 us
  transfers between devices with their start and end apart: 133, of which 114 were waited for; matrix products, arithmetic and copies ran while one was open for 4% of the time, Pallas kernels for 0%

profile of v1, /device:TPU:109, one launch (start us, length us, event | category | flops | bytes accessed | tf_op | source)
XLA Modules:
  0.0 1584.0 jit_solution(12952662461647068934)
XLA Ops:
  1.8 1582.2 %while.21 = (s32[]{:T(128)}, bf16[64,1024]{1,0:T(8,128)(2,1)S(1)}, bf16[4,64,1024]{2,1,0:T(8,128)(2,1)}, s32[]{:T(128)}, s32[4]{0:T(128)}, /*index=5*/pred[]{:T(...) while((s32[]{:T(128)}, bf16[64,1024]{1,0:T(8,128)(2,1)S(1)}, ...), condition=%wide.region_22.23_spmd.clone, body=%wide.region_0.22_spmd.clone.sunk | while | flops 1626031104 | bytes 78925872 | solution.py:186
  2.6 5.0 all-to-all-start
  11.8 4.7 all-to-all-start.1
  55.2 7.7 collective-permute-done.2
  71.2 4.6 all-to-all-start.1
  114.6 12.3 collective-permute-done.2
  135.2 4.6 all-to-all-start.1
  178.6 12.3 collective-permute-done.2
  199.1 4.6 all-to-all-start.1
  242.5 12.3 collective-permute-done.2
  263.1 4.6 all-to-all-start.1
  306.5 12.3 collective-permute-done.2
  327.0 4.6 all-to-all-start.1
  370.4 12.3 collective-permute-done.2
  391.0 4.6 all-to-all-start.1
  434.4 12.3 collective-permute-done.2
  498.3 12.3 collective-permute-done.2
  518.9 4.6 all-to-all-start.1
  562.3 12.3 collective-permute-done.2
  582.9 4.6 all-to-all-start.1
  626.2 12.3 collective-permute-done.2
  646.8 4.6 all-to-all-start.1
  690.2 12.3 collective-permute-done.2
  710.8 4.6 all-to-all-start.1
  754.2 12.4 collective-permute-done.2
  774.9 4.6 all-to-all-start.1
  818.4 12.4 collective-permute-done.2
  839.1 4.6 all-to-all-start.1
  882.5 12.3 collective-permute-done.2
  903.1 4.6 all-to-all-start.1
  946.5 291.1 %collective-permute-done.2 = bf16[64,1024]{1,0:T(8,128)(2,1)S(1)} collective-permute-done((bf16[64,1024]{1,0:T(8,128)(2,1)S(1)}, bf16[64,1024]{1,0:T(8,128)(2,1)S(1)}, u32[]{:S(2)}, u32[]{:S(2)}) %collective-permute-start.2) | collective-permute-done | bytes 131104 | tf_op jit(solution)/shard_map/while/body/eval_jaxpr/ppermute | solution.py:27
  1237.6 10.7 conditional.12
  1238.9 5.2 fusion.90
  1256.5 4.6 all-to-all-start.1
  1291.6 8.1 conditional.14
  1314.0 13.3 collective-permute-done.2
  1327.4 10.7 conditional.12
  1328.6 5.2 fusion.90
  1346.3 4.6 all-to-all-start.1
  1381.4 8.1 conditional.14
  1403.8 13.3 collective-permute-done.2
  1417.1 10.7 conditional.12
  1418.4 5.2 fusion.90
  1471.1 8.1 conditional.14
  1493.5 12.8 collective-permute-done.2
  1506.3 10.7 conditional.12
  1507.6 5.2 fusion.90
  1560.3 8.1 conditional.14
  (1302 shorter events, 1021.5 us)
Async XLA Ops:
  2.6 9.2 all-to-all-start
  11.8 8.9 all-to-all-start.1
  20.7 8.8 all-to-all-start.2
  53.2 9.7 collective-permute-start.2
  71.2 8.9 all-to-all-start.1
  80.1 8.8 all-to-all-start.2
  112.6 14.3 collective-permute-start.2
  135.2 8.9 all-to-all-start.1
  144.0 8.8 all-to-all-start.2
  176.6 14.3 collective-permute-start.2
  199.1 8.9 all-to-all-start.1
  208.0 8.8 all-to-all-start.2
  240.5 14.3 collective-permute-start.2
  263.1 8.9 all-to-all-start.1
  272.0 8.8 all-to-all-start.2
  304.5 14.3 collective-permute-start.2
  327.0 8.9 all-to-all-start.1
  335.9 8.8 all-to-all-start.2
  368.4 14.3 collective-permute-start.2
  391.0 8.9 all-to-all-start.1
  399.9 8.8 all-to-all-start.2
  432.4 14.3 collective-permute-start.2
  454.9 8.9 all-to-all-start.1
  463.8 8.8 all-to-all-start.2
  496.3 14.3 collective-permute-start.2
  518.9 8.9 all-to-all-start.1
  560.3 14.3 collective-permute-start.2
  582.9 8.9 all-to-all-start.1
  624.3 14.3 collective-permute-start.2
  646.8 8.9 all-to-all-start.1
  688.2 14.3 collective-permute-start.2
  710.8 8.9 all-to-all-start.1
  752.2 14.4 collective-permute-start.2
  774.9 8.9 all-to-all-start.1
  816.4 14.4 collective-permute-start.2
  839.1 8.9 all-to-all-start.1
  880.5 14.3 collective-permute-start.2
  903.1 8.9 all-to-all-start.1
  944.5 293.1 %collective-permute-start.2 = (bf16[64,1024]{1,0:T(8,128)(2,1)S(1)}, bf16[64,1024]{1,0:T(8,128)(2,1)S(1)}, u32[]{:S(2)}, u32[]{:S(2)}) collective-permute-start(bf16[64,1024]{1,0:T(8,128)(2,1)S(1)} %get-tuple-element.1116), channel_id=1, source_target_pairs={{0,8},{8,16},{16,24},{24,32},{32,40},{40,48},{48,56},{56,64},{64,7... | collective-permute-start | bytes 393224 | tf_op jit(solution)/shard_map/while/body/eval_jaxpr/ppermute | solution.py:27
  1256.5 8.9 all-to-all-start.1
  1265.4 8.9 all-to-all-start.2
  1282.7 8.9 all-to-all-start.3
  1312.0 15.3 collective-permute-start.2
  1346.3 8.9 all-to-all-start.1
  1401.8 15.3 collective-permute-start.2
  1436.0 8.9 all-to-all-start.1
  1491.5 14.8 collective-permute-start.2
  1525.2 8.9 all-to-all-start.1
  (219 other events, 2274.6 us)
